TPU v7x, 32 devices: a whole 2x2x4 slice. The times are simulated.
32 devices in a mesh: gx: 4 (over z), gy: 4 (over y, x), gz: 2 (over core).
Axes of the slice: x: 2, y: 2, z: 4, core: 2. Of those that a mesh axis runs over, the one named last changes fastest.
Arguments:
- signal: float32 [16, 131072], P(None, ('gx', 'gy', 'gz')), may hold values from -6 to 6
- order: int32 [131072], P(('gx', 'gy', 'gz')), may hold values from 0 to 4095, as said below
- near_tiles: bfloat16 [512, 3, 256, 256], P(('gx', 'gy', 'gz')), may hold values from -0.21875 to 0.21875
- near_list: int32 [512, 3], P(('gx', 'gy', 'gz')), may hold values from 0 to 511, as said below
- leaf_basis: bfloat16 [512, 64, 256], P(('gx', 'gy', 'gz')), may hold values from -0.375 to 0.375
- leaf_transfer: bfloat16 [512, 64, 64], P(('gx', 'gy', 'gz')), may hold values from -0.5 to 0.5
- leaf_coupling: bfloat16 [512, 64, 192], P(('gx', 'gy', 'gz')), may hold values from -0.4375 to 0.4375
- leaf_links: int32 [512, 3], P(('gx', 'gy', 'gz')), may hold values from 0 to 511, as said below
- device_transfer: bfloat16 [32, 64, 64], P(('gx', 'gy', 'gz')), may hold values from -0.5 to 0.5
- device_coupling: bfloat16 [32, 64, 192], P(('gx', 'gy', 'gz')), may hold values from -0.15625 to 0.15625
- device_links: int32 [32, 3], P(('gx', 'gy', 'gz')), may hold values from 0 to 31, as said below
- block_transfer: bfloat16 [16, 64, 64], P(('gx', 'gy')), may hold values from -0.5 to 0.5
- block_coupling: bfloat16 [16, 64, 192], P(('gx', 'gy')), may hold values from -0.15625 to 0.15625
- block_links: int32 [16, 3], P(('gx', 'gy')), may hold values from 0 to 15, as said below
- top_coupling: bfloat16 [4, 64, 192], P('gx'), may hold values from -0.109375 to 0.109375
- top_links: int32 [4, 3], P('gx'), may hold values from 0 to 3, as said below
Outputs:
- smoothed: float32 [16, 131072], P(None, ('gx', 'gy', 'gz'))
- twice: float32 [16, 131072], P(None, ('gx', 'gy', 'gz'))
Inputs may be any that keep to these rules, and one draw needn't show every extreme that they name: `order`: each device's block of 4096 consecutive entries is a permutation of 0 to 4095. `near_list`: row i holds i first, then two different leaves j with 1 <= |j - i| <= 2. `leaf_links`: row i holds three different leaves j with 2 <= |j - i| <= 4. `device_links`: row i holds three different device clusters j with 1 <= |j - i| <= 3. `block_links`: row i holds three different second-level clusters other than i. `top_links`: row i holds three different first-level clusters other than i.
All inputs are finite; a program needn't handle non-finite values.
Results may differ from a plain program's by a relative error of at most 0.0043.
Values may be sent and summed in bfloat16 or wider, within the bound.
No kernel may reach another device: no remote copies, remote signals or barrier semaphores. Data moves between devices by JAX's collectives and lax.ppermute only.
A program may use at most 64 MiB of HBM per device.

v0:
```python
import jax
import jax.numpy as jnp
from jax import lax
from jax.sharding import PartitionSpec as P

NEAR_REACH = 2
LINK_REACH = 4
DEVICE_REACH = 3
HIGH = lax.Precision.HIGHEST


def shifted(block, axis, distance):
    devices = range(lax.axis_size(axis))
    route = [(i - distance, i) for i in devices if i - distance in devices]
    return lax.ppermute(block, axis, route)


def couple(picked, coupling):
    rank_dim = coupling.shape[0]
    link_count = picked.shape[0]
    table = coupling.astype(jnp.float32).reshape(rank_dim, link_count, rank_dim)
    return jnp.einsum("jrk,kjm->rm", picked, table, precision=HIGH)


def spread_down(parent, transfer):
    return jnp.dot(parent, transfer.astype(jnp.float32).T, precision=HIGH)


def relay_side(own_moment, direction):
    window = own_moment[None][:0]
    for step in range(DEVICE_REACH):
        outgoing = jnp.concatenate([own_moment[None], window], axis=0)
        window = shifted(outgoing, ("gx", "gy", "gz"), direction)
    return window


def apply_matrix(
    leaves,
    near_tiles,
    near_list,
    leaf_basis,
    leaf_transfer,
    leaf_coupling,
    leaf_links,
    device_transfer,
    device_coupling,
    device_links,
    block_transfer,
    block_coupling,
    block_links,
    top_coupling,
    top_links,
):
    leaf_dev = leaves.shape[1]
    device = lax.axis_index(("gx", "gy", "gz"))
    first_leaf = device * leaf_dev
    rims = []
    for offset, edge in ((1, leaves[:, leaf_dev - NEAR_REACH :]), (-1, leaves[:, :NEAR_REACH])):
        rims.append(shifted(edge, ("gx", "gy", "gz"), offset))
    widened = jnp.concatenate([rims[0], leaves, rims[1]], axis=1)
    moments = jnp.einsum("rls,lks->rlk", leaves, leaf_basis, preferred_element_type=jnp.float32)
    edges = []
    for offset, edge in ((1, moments[:, leaf_dev - LINK_REACH :]), (-1, moments[:, :LINK_REACH])):
        edges.append(shifted(edge, ("gx", "gy", "gz"), offset))
    wide_moments = jnp.concatenate([edges[0], moments, edges[1]], axis=1)
    transfer_f = leaf_transfer.astype(jnp.float32)
    own_moment = jnp.einsum("rlk,lkm->rm", moments, transfer_f, precision=HIGH)
    block_term = jnp.dot(own_moment, device_transfer[0].astype(jnp.float32), precision=HIGH)
    block_moment = lax.psum(block_term, "gz")
    lower = relay_side(own_moment, 1)
    upper = relay_side(own_moment, -1)
    stacked = jnp.concatenate([lower[::-1], upper], axis=0)
    relative = device_links[0] - device
    position = relative + DEVICE_REACH - (relative > 0).astype(jnp.int32)
    device_picked = stacked[position]
    top_term = jnp.dot(block_moment, block_transfer[0].astype(jnp.float32), precision=HIGH)
    top_moment = lax.psum(top_term, "gy")
    every_top = lax.all_gather(top_moment[None], "gx", axis=0, tiled=True)
    every_block = lax.all_gather(block_moment[None], ("gx", "gy"), axis=0, tiled=True)
    top_field = couple(every_top[top_links[0]], top_coupling[0])
    block_field = couple(every_block[block_links[0]], block_coupling[0]) + spread_down(
        top_field, block_transfer[0]
    )
    device_field = couple(device_picked, device_coupling[0]) + spread_down(
        block_field, device_transfer[0]
    )
    local_links = leaf_links - first_leaf + LINK_REACH
    picked = wide_moments[:, local_links]
    rank_dim = leaf_coupling.shape[1]
    leaf_table = leaf_coupling.astype(jnp.float32).reshape(leaf_dev, rank_dim, -1, rank_dim)
    leaf_field = jnp.einsum("rljk,lkjm->rlm", picked, leaf_table, precision=HIGH)
    leaf_field = leaf_field + jnp.einsum("rm,lkm->rlk", device_field, transfer_f, precision=HIGH)
    far_part = jnp.einsum(
        "rlk,lks->rls",
        leaf_field.astype(jnp.bfloat16),
        leaf_basis,
        preferred_element_type=jnp.float32,
    )
    near_index = near_list - first_leaf + NEAR_REACH
    near_rows = widened[:, near_index]
    near_part = jnp.einsum(
        "rlns,lnst->rlt", near_rows, near_tiles, preferred_element_type=jnp.float32
    )
    return near_part + far_part


def shards(
    signal,
    order,
    near_tiles,
    near_list,
    leaf_basis,
    leaf_transfer,
    leaf_coupling,
    leaf_links,
    device_transfer,
    device_coupling,
    device_links,
    block_transfer,
    block_coupling,
    block_links,
    top_coupling,
    top_links,
):
    matrices = (
        near_tiles,
        near_list,
        leaf_basis,
        leaf_transfer,
        leaf_coupling,
        leaf_links,
        device_transfer,
        device_coupling,
        device_links,
        block_transfer,
        block_coupling,
        block_links,
        top_coupling,
        top_links,
    )
    rhs_count = signal.shape[0]
    leaf_count = near_tiles.shape[0]
    tree = jnp.take(signal, order, axis=1).astype(jnp.bfloat16).reshape(rhs_count, leaf_count, -1)
    first = apply_matrix(tree, *matrices)
    second = apply_matrix(first.astype(jnp.bfloat16), *matrices)
    empty = jnp.zeros_like(signal)
    smoothed = empty.at[:, order].set(first.reshape(rhs_count, -1))
    twice = empty.at[:, order].set(second.reshape(rhs_count, -1))
    return (smoothed, twice)


def solution(mesh):
    in_specs = (
        P(None, ("gx", "gy", "gz")),
        P(("gx", "gy", "gz")),
        P(("gx", "gy", "gz"), None, None, None),
        P(("gx", "gy", "gz"), None),
        P(("gx", "gy", "gz"), None, None),
        P(("gx", "gy", "gz"), None, None),
        P(("gx", "gy", "gz"), None, None),
        P(("gx", "gy", "gz"), None),
        P(("gx", "gy", "gz"), None, None),
        P(("gx", "gy", "gz"), None, None),
        P(("gx", "gy", "gz"), None),
        P(("gx", "gy"), None, None),
        P(("gx", "gy"), None, None),
        P(("gx", "gy"), None),
        P("gx", None, None),
        P("gx", None),
    )
    out_specs = (P(None, ("gx", "gy", "gz")), P(None, ("gx", "gy", "gz")))
    return jax.shard_map(shards, mesh=mesh, in_specs=in_specs, out_specs=out_specs, check_vma=False)
```

profile of v0, /device:TPU:4, one launch (start us, length us, event | category | flops | bytes accessed | tf_op | source)
XLA Modules:
  0.0 253.0 jit_solution(4829175544819906488)
XLA Ops:
  0.6 0.8 compare_and_fusion
  1.4 1.3 broadcast_clamp_fusion
  2.8 1.5 copy.38
  4.4 12.1 %gather_fusion = bf16[4096,16]{1,0:T(8,128)(2,1)S(1)} fusion(bf16[16,4096]{0,1:T(8,128)(2,1)S(1)} %copy.38, s32[4096]{0:T(1024)S(1)} %get-tuple-element.16), kind=kCustom, calls=%fused_computation | custom fusion | bytes 278528 | tf_op jit(solution)/shard_map/jit(_take)/gather | solution.py:143
  16.5 0.3 copy.39
  17.1 0.3 fusion.36
  17.4 2.8 %collective-permute-start.7 = (f32[1,16,64]{2,1,0:T(8,128)S(1)}, f32[1,16,64]{2,1,0:T(8,128)S(1)}, u32[]{:S(2)}, u32[]{:S(2)}) collective-permute-start(f32[1,16,64]{2,1,0:T(8,128)S(1)} %bitcast.193), channel_id=1, source_target_pairs={{1,0},{2,1},{3,2},{4,3},{5,4},{6,5},{7,6},{8,7},{9,8},{10,9},{11,1... | collective-permute-start | bytes 12296 | tf_op jit(solution)/shard_map/ppermute | solution.py:15
  20.2 1.9 collective-permute-start.4
  22.2 2.6 %collective-permute-start = (bf16[16,2,256]{2,0,1:T(8,128)(2,1)S(1)}, bf16[16,2,256]{2,0,1:T(8,128)(2,1)S(1)}, u32[]{:S(2)}, u32[]{:S(2)}) collective-permute-start(bf16[16,2,256]{2,0,1:T(8,128)(2,1)S(1)} %get-tuple-element.14), channel_id=1, source_target_pairs={{0,1},{1,2},{2,3},{3,4},{4,5},{5,6},{6,7},{7,8},{8,9},{9,10},{10,1... | collective-permute-start | bytes 49160 | tf_op jit(solution)/shard_map/ppermute | solution.py:15
  24.8 3.8 %collective-permute-start.1 = (bf16[16,2,256]{2,0,1:T(8,128)(2,1)S(1)}, bf16[16,2,256]{2,0,1:T(8,128)(2,1)S(1)}, u32[]{:S(2)}, u32[]{:S(2)}) collective-permute-start(bf16[16,2,256]{2,0,1:T(8,128)(2,1)S(1)} %get-tuple-element.15), channel_id=1, source_target_pairs={{1,0},{2,1},{3,2},{4,3},{5,4},{6,5},{7,6},{8,7},{9,8},{10,9},{11,1... | collective-permute-start | bytes 49160 | tf_op jit(solution)/shard_map/ppermute | solution.py:15
  28.6 1.9 collective-permute-start.2
  31.3 3.6 %psum.28 = f32[16,64]{1,0:T(8,128)S(1)} all-reduce(f32[16,64]{1,0:T(8,128)S(1)} %fusion.23), channel_id=1, replica_groups=mesh['gx'=4,'gy'=4,'gz'=2] {'gz'}, use_global_device_ids=true, to_apply=%region_0.1 | all-reduce | flops 1024 | bytes 8192 | tf_op jit(solution)/shard_map/psum | solution.py:69
  34.9 35.5 %all-gather = f32[256,64]{1,0:T(8,128)S(1)} all-gather(f32[16,64]{1,0:T(8,128)S(1)} %psum.28), channel_id=2, replica_groups=mesh['gx'=4,'gy'=4,'gz'=2] {'gx','gy'}, dimensions={0}, use_global_device_ids=true | all-gather | bytes 69632 | tf_op jit(solution)/shard_map/all_gather | solution.py:79
  70.6 10.2 %psum.29 = f32[1,16,64]{2,1,0:T(8,128)S(1)} all-reduce(f32[1,16,64]{2,1,0:T(8,128)S(1)} %convolution_bitcast_fusion.11), channel_id=1, replica_groups=mesh['gx'=4,'gy'=4,'gz'=2] {'gy'}, use_global_device_ids=true, to_apply=%region_1.2 | all-reduce | flops 1024 | bytes 8192 | tf_op jit(solution)/shard_map/psum | solution.py:77
  80.8 13.1 %all_gather.13 = f32[4,16,64]{2,1,0:T(8,128)S(1)} all-gather(f32[1,16,64]{2,1,0:T(8,128)S(1)} %psum.29), channel_id=1, replica_groups=mesh['gx'=4,'gy'=4,'gz'=2] {'gx'}, dimensions={0}, use_global_device_ids=true | all-gather | bytes 20480 | tf_op jit(solution)/shard_map/all_gather | solution.py:78
  93.9 0.5 gather_fusion.5
  94.6 0.6 gather_fusion.4
  95.9 1.9 collective-permute-start.5
  97.8 4.5 %collective-permute-start.8 = (f32[2,16,64]{2,1,0:T(8,128)S(1)}, f32[2,16,64]{2,1,0:T(8,128)S(1)}, u32[]{:S(2)}, u32[]{:S(2)}) collective-permute-start(f32[2,16,64]{2,1,0:T(8,128)S(1)} %get-tuple-element.25), channel_id=1, source_target_pairs={{1,0},{2,1},{3,2},{4,3},{5,4},{6,5},{7,6},{8,7},{9,8},{10,9},{11,1... | collective-permute-start | bytes 24584 | tf_op jit(solution)/shard_map/ppermute | solution.py:15
  102.6 0.4 copy.42
  103.0 2.3 collective-permute-start.3
  105.3 2.0 collective-permute-start.6
  107.3 4.4 %collective-permute-start.9 = (f32[3,16,64]{2,1,0:T(8,128)S(1)}, f32[3,16,64]{2,1,0:T(8,128)S(1)}, u32[]{:S(2)}, u32[]{:S(2)}) collective-permute-start(f32[3,16,64]{2,1,0:T(8,128)S(1)} %get-tuple-element.23), channel_id=1, source_target_pairs={{1,0},{2,1},{3,2},{4,3},{5,4},{6,5},{7,6},{8,7},{9,8},{10,9},{11,1... | collective-permute-start | bytes 36872 | tf_op jit(solution)/shard_map/ppermute | solution.py:15
  111.8 0.6 gather_fusion.1
  112.4 3.7 %convolution_bitcast_fusion.1 = f32[16,16,256]{2,1,0:T(8,128)S(1)} fusion(bf16[16,16,3,256]{3,0,2,1:T(8,128)(2,1)S(1)} %bitcast.178, bf16[16,3,256,256]{3,2,1,0:T(8,128)(2,1)} %param.18), kind=kOutput, calls=%fused_computation.17 | convolution fusion | flops 100663296 | bytes 6946816 | tf_op jit(solution)/shard_map/rlns,lnst->rlt/dot_general | solution.py:101
  116.2 0.6 gather_fusion.2
  116.9 0.6 gather_fusion.3
  117.6 0.7 fusion.37
  118.3 0.9 fusion.3
  119.5 0.6 fusion.33
  120.8 1.9 collective-permute-start.17
  122.7 2.4 collective-permute-start.14
  125.1 0.6 fusion.32
  125.8 2.5 psum.30
  128.3 34.8 %all-gather.1 = f32[256,64]{1,0:T(8,128)S(1)} all-gather(f32[16,64]{1,0:T(8,128)S(1)} %psum.30), channel_id=3, replica_groups=mesh['gx'=4,'gy'=4,'gz'=2] {'gx','gy'}, dimensions={0}, use_global_device_ids=true | all-gather | bytes 69632 | tf_op jit(solution)/shard_map/all_gather | solution.py:79
  163.1 1.9 collective-permute-start.10
  165.0 4.5 %collective-permute-start.11 = (bf16[16,2,256]{2,0,1:T(8,128)(2,1)}, bf16[16,2,256]{2,0,1:T(8,128)(2,1)}, u32[]{:S(2)}, u32[]{:S(2)}) collective-permute-start(bf16[16,2,256]{2,0,1:T(8,128)(2,1)} %get-tuple-element.11), channel_id=1, source_target_pairs={{1,0},{2,1},{3,2},{4,3},{5,4},{6,5},{7,6},{8,7},{9,8},{10,9},{11,1... | collective-permute-start | bytes 49160 | tf_op jit(solution)/shard_map/ppermute | solution.py:15
  169.6 10.1 %psum.31 = f32[1,16,64]{2,1,0:T(8,128)S(1)} all-reduce(f32[1,16,64]{2,1,0:T(8,128)S(1)} %convolution_bitcast_fusion.7), channel_id=1, replica_groups=mesh['gx'=4,'gy'=4,'gz'=2] {'gy'}, use_global_device_ids=true, to_apply=%region_4.5 | all-reduce | flops 1024 | bytes 8192 | tf_op jit(solution)/shard_map/psum | solution.py:77
  179.7 13.1 %all_gather.15 = f32[4,16,64]{2,1,0:T(8,128)S(1)} all-gather(f32[1,16,64]{2,1,0:T(8,128)S(1)} %psum.31), channel_id=1, replica_groups=mesh['gx'=4,'gy'=4,'gz'=2] {'gx'}, dimensions={0}, use_global_device_ids=true | all-gather | bytes 20480 | tf_op jit(solution)/shard_map/all_gather | solution.py:78
  192.9 0.5 gather_fusion.10
  193.6 1.9 collective-permute-start.12
  195.5 0.6 gather_fusion.9
  196.4 0.6 pad_maximum_fusion.13
  197.0 1.9 collective-permute-start.15
  198.9 4.5 %collective-permute-start.18 = (f32[2,16,64]{2,1,0:T(8,128)}, f32[2,16,64]{2,1,0:T(8,128)}, u32[]{:S(2)}, u32[]{:S(2)}) collective-permute-start(f32[2,16,64]{2,1,0:T(8,128)} %get-tuple-element.21), channel_id=1, source_target_pairs={{1,0},{2,1},{3,2},{4,3},{5,4},{6,5},{7,6},{8,7},{9,8},{10,9},{11,1... | collective-permute-start | bytes 24584 | tf_op jit(solution)/shard_map/ppermute | solution.py:15
  203.5 0.8 fusion.17
  204.3 2.0 copy.51
  206.2 11.4 %scatter_custom_fusion = f32[16,4096]{0,1:T(8,128)S(1)} fusion(s32[4096]{0:T(1024)} %get-tuple-element.17, f32[4096,16]{1,0:T(8,128)} %copy.51, f32[]{:T(128)} %constant.15.clone.1), kind=kCustom, calls=%fused_computation.42 | custom fusion | bytes 262656 | tf_op jit(solution)/shard_map/scatter | solution.py:147
  217.7 1.3 copy.58
  218.9 2.4 collective-permute-start.13
  221.4 0.7 pad_maximum_fusion.9
  222.1 1.9 collective-permute-start.16
  224.0 4.7 %collective-permute-start.19 = (f32[3,16,64]{2,1,0:T(8,128)S(1)}, f32[3,16,64]{2,1,0:T(8,128)S(1)}, u32[]{:S(2)}, u32[]{:S(2)}) collective-permute-start(f32[3,16,64]{2,1,0:T(8,128)S(1)} %get-tuple-element.19), channel_id=1, source_target_pairs={{1,0},{2,1},{3,2},{4,3},{5,4},{6,5},{7,6},{8,7},{9,8},{10,9},{11,1... | collective-permute-start | bytes 36872 | tf_op jit(solution)/shard_map/ppermute | solution.py:15
  228.8 0.9 pad_maximum_fusion.3
  229.7 0.6 gather_fusion.6
  230.4 3.8 %convolution_bitcast_fusion = f32[16,16,256]{2,1,0:T(8,128)S(1)} fusion(bf16[16,16,3,256]{3,0,2,1:T(8,128)(2,1)S(1)} %bitcast.177, bf16[16,3,256,256]{3,2,1,0:T(8,128)(2,1)} %param.18), kind=kOutput, calls=%fused_computation.15 | convolution fusion | flops 100663296 | bytes 6946816 | tf_op jit(solution)/shard_map/rlns,lnst->rlt/dot_general | solution.py:101
  234.1 0.8 pad_maximum_fusion.1
  234.9 0.6 gather_fusion.7
  235.6 0.7 gather_fusion.8
  236.5 0.7 fusion.39
  237.2 0.9 fusion.4
  238.3 2.0 copy.57
  240.3 11.4 %scatter_custom_fusion.1 = f32[16,4096]{0,1:T(8,128)S(1)} fusion(s32[4096]{0:T(1024)} %get-tuple-element.17, f32[4096,16]{1,0:T(8,128)} %copy.57, f32[]{:T(128)} %constant.15.clone.1), kind=kCustom, calls=%fused_computation.40 | custom fusion | bytes 262656 | tf_op jit(solution)/shard_map/scatter | solution.py:148
  251.7 1.3 copy.59
  (120 shorter events, 4.1 us)
Async XLA Ops:
  0.6 16.3 %copy-start = (bf16[16,64,256]{2,1,0:T(8,128)(2,1)S(1)}, bf16[16,64,256]{2,1,0:T(8,128)(2,1)}, u32[]{:S(2)}) copy-start(bf16[16,64,256]{2,1,0:T(8,128)(2,1)} %param.20) | copy-start | bytes 1572868
  2.8 14.4 %copy-start.1 = (bf16[16,64,64]{2,1,0:T(8,128)(2,1)S(1)}, bf16[16,64,64]{2,1,0:T(8,128)(2,1)}, u32[]{:S(2)}) copy-start(bf16[16,64,64]{2,1,0:T(8,128)(2,1)} %param.21) | copy-start | bytes 393220
  4.2 26.3 %copy-start.23 = (s32[1,3]{1,0:T(1,128)S(1)}, s32[1,3]{1,0:T(1,128)}, u32[]{:S(2)}) copy-start(s32[1,3]{1,0:T(1,128)} %param.26) | copy-start | bytes 40
  4.3 26.3 %copy-start.24 = (s32[1,3]{1,0:T(1,128)S(1)}, s32[1,3]{1,0:T(1,128)}, u32[]{:S(2)}) copy-start(s32[1,3]{1,0:T(1,128)} %param.29) | copy-start | bytes 40
  4.3 26.4 %copy-start.25 = (s32[1,3]{1,0:T(1,128)S(1)}, s32[1,3]{1,0:T(1,128)}, u32[]{:S(2)}) copy-start(s32[1,3]{1,0:T(1,128)} %param.31) | copy-start | bytes 40
  4.3 26.4 %copy-start.21 = (s32[16,3]{0,1:T(4,128)S(1)}, s32[16,3]{0,1:T(4,128)}, u32[]{:S(2)}) copy-start(s32[16,3]{0,1:T(4,128)} %param.23) | copy-start | bytes 580
  4.3 26.4 %copy-start.22 = (s32[16,3]{0,1:T(4,128)S(1)}, s32[16,3]{0,1:T(4,128)}, u32[]{:S(2)}) copy-start(s32[16,3]{0,1:T(4,128)} %param.19) | copy-start | bytes 580
  4.3 26.6 %copy-start.16 = (bf16[1,64,192]{2,1,0:T(8,128)(2,1)S(1)}, bf16[1,64,192]{2,1,0:T(8,128)(2,1)}, u32[]{:S(2)}) copy-start(bf16[1,64,192]{2,1,0:T(8,128)(2,1)} %param.28) | copy-start | bytes 73732
  4.3 26.7 %copy-start.17 = (bf16[1,64,192]{2,1,0:T(8,128)(2,1)S(1)}, bf16[1,64,192]{2,1,0:T(8,128)(2,1)}, u32[]{:S(2)}) copy-start(bf16[1,64,192]{2,1,0:T(8,128)(2,1)} %param.30) | copy-start | bytes 73732
  4.3 26.8 %copy-start.8 = (bf16[1,64,64]{2,1,0:T(8,128)(2,1)S(1)}, bf16[1,64,64]{2,1,0:T(8,128)(2,1)}, u32[]{:S(2)}) copy-start(bf16[1,64,64]{2,1,0:T(8,128)(2,1)} %param.24) | copy-start | bytes 24580
  4.3 66.1 %copy-start.7 = (bf16[1,64,64]{2,1,0:T(8,128)(2,1)S(1)}, bf16[1,64,64]{2,1,0:T(8,128)(2,1)}, u32[]{:S(2)}) copy-start(bf16[1,64,64]{2,1,0:T(8,128)(2,1)} %param.27) | copy-start | bytes 24580
  16.5 85.9 %copy-start.18 = (bf16[1,64,192]{2,1,0:T(8,128)(2,1)S(1)}, bf16[1,64,192]{2,1,0:T(8,128)(2,1)}, u32[]{:S(2)}) copy-start(bf16[1,64,192]{2,1,0:T(8,128)(2,1)} %param.25) | copy-start | bytes 73732
  16.5 86.0 %copy-start.4 = (bf16[16,64,192]{2,1,0:T(8,128)(2,1)S(1)}, bf16[16,64,192]{2,1,0:T(8,128)(2,1)}, u32[]{:S(2)}) copy-start(bf16[16,64,192]{2,1,0:T(8,128)(2,1)} %param.22) | copy-start | bytes 1179652
  17.4 78.5 %collective-permute-start.7 = (f32[1,16,64]{2,1,0:T(8,128)S(1)}, f32[1,16,64]{2,1,0:T(8,128)S(1)}, u32[]{:S(2)}, u32[]{:S(2)}) collective-permute-start(f32[1,16,64]{2,1,0:T(8,128)S(1)} %bitcast.193), channel_id=1, source_target_pairs={{1,0},{2,1},{3,2},{4,3},{5,4},{6,5},{7,6},{8,7},{9,8},{10,9},{11,1... | collective-permute-start | bytes 12296 | tf_op jit(solution)/shard_map/ppermute | solution.py:15
  20.2 75.7 %collective-permute-start.4 = (f32[1,16,64]{2,1,0:T(8,128)S(1)}, f32[1,16,64]{2,1,0:T(8,128)S(1)}, u32[]{:S(2)}, u32[]{:S(2)}) collective-permute-start(f32[1,16,64]{2,1,0:T(8,128)S(1)} %bitcast.194), channel_id=1, source_target_pairs={{0,1},{1,2},{2,3},{3,4},{4,5},{5,6},{6,7},{7,8},{8,9},{9,10},{10,1... | collective-permute-start | bytes 12296 | tf_op jit(solution)/shard_map/ppermute | solution.py:15
  22.2 85.2 %collective-permute-start = (bf16[16,2,256]{2,0,1:T(8,128)(2,1)S(1)}, bf16[16,2,256]{2,0,1:T(8,128)(2,1)S(1)}, u32[]{:S(2)}, u32[]{:S(2)}) collective-permute-start(bf16[16,2,256]{2,0,1:T(8,128)(2,1)S(1)} %get-tuple-element.14), channel_id=1, source_target_pairs={{0,1},{1,2},{2,3},{3,4},{4,5},{5,6},{6,7},{7,8},{8,9},{9,10},{10,1... | collective-permute-start | bytes 49160 | tf_op jit(solution)/shard_map/ppermute | solution.py:15
  24.8 87.0 %collective-permute-start.1 = (bf16[16,2,256]{2,0,1:T(8,128)(2,1)S(1)}, bf16[16,2,256]{2,0,1:T(8,128)(2,1)S(1)}, u32[]{:S(2)}, u32[]{:S(2)}) collective-permute-start(bf16[16,2,256]{2,0,1:T(8,128)(2,1)S(1)} %get-tuple-element.15), channel_id=1, source_target_pairs={{1,0},{2,1},{3,2},{4,3},{5,4},{6,5},{7,6},{8,7},{9,8},{10,9},{11,1... | collective-permute-start | bytes 49160 | tf_op jit(solution)/shard_map/ppermute | solution.py:15
  28.6 87.5 %collective-permute-start.2 = (f32[16,4,64]{2,0,1:T(8,128)S(1)}, f32[16,4,64]{2,0,1:T(8,128)S(1)}, u32[]{:S(2)}, u32[]{:S(2)}) collective-permute-start(f32[16,4,64]{2,0,1:T(8,128)S(1)} %get-tuple-element.12), channel_id=1, source_target_pairs={{0,1},{1,2},{2,3},{3,4},{4,5},{5,6},{6,7},{7,8},{8,9},{9,10},{10,1... | collective-permute-start | bytes 49160 | tf_op jit(solution)/shard_map/ppermute | solution.py:15
  30.7 86.1 %copy-start.20 = (s32[1024]{0:T(1024)}, s32[1024]{0:T(1024)S(1)}, u32[]{:S(2)}) copy-start(s32[1024]{0:T(1024)S(1)} %pad_clamp_fusion.2) | copy-start | bytes 12292
  95.7 20.5 %copy-start.12 = (s32[1024]{0:T(1024)}, s32[1024]{0:T(1024)S(1)}, u32[]{:S(2)}) copy-start(s32[1024]{0:T(1024)S(1)} %pad_clamp_fusion.3) | copy-start | bytes 12292
  95.9 7.0 %collective-permute-start.5 = (f32[2,16,64]{2,1,0:T(8,128)S(1)}, f32[2,16,64]{2,1,0:T(8,128)S(1)}, u32[]{:S(2)}, u32[]{:S(2)}) collective-permute-start(f32[2,16,64]{2,1,0:T(8,128)S(1)} %get-tuple-element.24), channel_id=1, source_target_pairs={{0,1},{1,2},{2,3},{3,4},{4,5},{5,6},{6,7},{7,8},{8,9},{9,10},{10,1... | collective-permute-start | bytes 24584 | tf_op jit(solution)/shard_map/ppermute | solution.py:15
  97.8 7.4 %collective-permute-start.8 = (f32[2,16,64]{2,1,0:T(8,128)S(1)}, f32[2,16,64]{2,1,0:T(8,128)S(1)}, u32[]{:S(2)}, u32[]{:S(2)}) collective-permute-start(f32[2,16,64]{2,1,0:T(8,128)S(1)} %get-tuple-element.25), channel_id=1, source_target_pairs={{1,0},{2,1},{3,2},{4,3},{5,4},{6,5},{7,6},{8,7},{9,8},{10,9},{11,1... | collective-permute-start | bytes 24584 | tf_op jit(solution)/shard_map/ppermute | solution.py:15
  102.4 13.7 %copy-start.14 = (s32[1024]{0:T(1024)}, s32[1024]{0:T(1024)S(1)}, u32[]{:S(2)}) copy-start(s32[1024]{0:T(1024)S(1)} %pad_clamp_fusion.4) | copy-start | bytes 12292
  102.6 14.9 %copy-start.5 = (bf16[1,64,192]{1,2,0:T(8,128)(2,1)}, bf16[1,64,192]{1,2,0:T(8,128)(2,1)S(1)}, u32[]{:S(2)}) copy-start(bf16[1,64,192]{1,2,0:T(8,128)(2,1)S(1)} %copy.44) | copy-start | bytes 73732
  103.0 13.2 %collective-permute-start.3 = (f32[16,4,64]{2,0,1:T(8,128)S(1)}, f32[16,4,64]{2,0,1:T(8,128)S(1)}, u32[]{:S(2)}, u32[]{:S(2)}) collective-permute-start(f32[16,4,64]{2,0,1:T(8,128)S(1)} %get-tuple-element.13), channel_id=1, source_target_pairs={{1,0},{2,1},{3,2},{4,3},{5,4},{6,5},{7,6},{8,7},{9,8},{10,9},{11,1... | collective-permute-start | bytes 49160 | tf_op jit(solution)/shard_map/ppermute | solution.py:15
  105.3 11.5 %collective-permute-start.6 = (f32[3,16,64]{2,1,0:T(8,128)S(1)}, f32[3,16,64]{2,1,0:T(8,128)S(1)}, u32[]{:S(2)}, u32[]{:S(2)}) collective-permute-start(f32[3,16,64]{2,1,0:T(8,128)S(1)} %get-tuple-element.22), channel_id=1, source_target_pairs={{0,1},{1,2},{2,3},{3,4},{4,5},{5,6},{6,7},{7,8},{8,9},{9,10},{10,1... | collective-permute-start | bytes 36872 | tf_op jit(solution)/shard_map/ppermute | solution.py:15
  107.3 9.5 %collective-permute-start.9 = (f32[3,16,64]{2,1,0:T(8,128)S(1)}, f32[3,16,64]{2,1,0:T(8,128)S(1)}, u32[]{:S(2)}, u32[]{:S(2)}) collective-permute-start(f32[3,16,64]{2,1,0:T(8,128)S(1)} %get-tuple-element.23), channel_id=1, source_target_pairs={{1,0},{2,1},{3,2},{4,3},{5,4},{6,5},{7,6},{8,7},{9,8},{10,9},{11,1... | collective-permute-start | bytes 36872 | tf_op jit(solution)/shard_map/ppermute | solution.py:15
  117.6 3.0 %copy-start.9 = (bf16[1,64,64]{2,1,0:T(8,128)(2,1)S(1)}, bf16[1,64,64]{2,1,0:T(8,128)(2,1)}, u32[]{:S(2)}) copy-start(bf16[1,64,64]{2,1,0:T(8,128)(2,1)} %param.24) | copy-start | bytes 24580
  119.5 86.8 %copy-start.3 = (bf16[16,16,256]{2,0,1:T(8,128)(2,1)}, bf16[16,16,256]{2,0,1:T(8,128)(2,1)S(1)}, u32[]{:S(2)}) copy-start(bf16[16,16,256]{2,0,1:T(8,128)(2,1)S(1)} %get-tuple-element.26) | copy-start | bytes 393220
  120.6 83.6 %copy-start.10 = (f32[16,64,1]{1,0,2:T(8,128)}, f32[16,64,1]{1,0,2:T(8,128)S(1)}, u32[]{:S(2)}) copy-start(f32[16,64,1]{1,0,2:T(8,128)S(1)} %fusion.38) | copy-start | bytes 12292
  120.8 75.6 %collective-permute-start.17 = (f32[1,16,64]{2,1,0:T(8,128)S(1)}, f32[1,16,64]{2,1,0:T(8,128)S(1)}, u32[]{:S(2)}, u32[]{:S(2)}) collective-permute-start(f32[1,16,64]{2,1,0:T(8,128)S(1)} %bitcast.197), channel_id=1, source_target_pairs={{1,0},{2,1},{3,2},{4,3},{5,4},{6,5},{7,6},{8,7},{9,8},{10,9},{11,1... | collective-permute-start | bytes 12296 | tf_op jit(solution)/shard_map/ppermute | solution.py:15
  122.7 73.7 %collective-permute-start.14 = (f32[1,16,64]{2,1,0:T(8,128)S(1)}, f32[1,16,64]{2,1,0:T(8,128)S(1)}, u32[]{:S(2)}, u32[]{:S(2)}) collective-permute-start(f32[1,16,64]{2,1,0:T(8,128)S(1)} %bitcast.198), channel_id=1, source_target_pairs={{0,1},{1,2},{2,3},{3,4},{4,5},{5,6},{6,7},{7,8},{8,9},{9,10},{10,1... | collective-permute-start | bytes 12296 | tf_op jit(solution)/shard_map/ppermute | solution.py:15
  163.1 60.9 %collective-permute-start.10 = (bf16[16,2,256]{2,0,1:T(8,128)(2,1)}, bf16[16,2,256]{2,0,1:T(8,128)(2,1)}, u32[]{:S(2)}, u32[]{:S(2)}) collective-permute-start(bf16[16,2,256]{2,0,1:T(8,128)(2,1)} %get-tuple-element.10), channel_id=1, source_target_pairs={{0,1},{1,2},{2,3},{3,4},{4,5},{5,6},{6,7},{7,8},{8,9},{9,10},{10,1... | collective-permute-start | bytes 49160 | tf_op jit(solution)/shard_map/ppermute | solution.py:15
  165.0 63.8 %collective-permute-start.11 = (bf16[16,2,256]{2,0,1:T(8,128)(2,1)}, bf16[16,2,256]{2,0,1:T(8,128)(2,1)}, u32[]{:S(2)}, u32[]{:S(2)}) collective-permute-start(bf16[16,2,256]{2,0,1:T(8,128)(2,1)} %get-tuple-element.11), channel_id=1, source_target_pairs={{1,0},{2,1},{3,2},{4,3},{5,4},{6,5},{7,6},{8,7},{9,8},{10,9},{11,1... | collective-permute-start | bytes 49160 | tf_op jit(solution)/shard_map/ppermute | solution.py:15
  193.6 40.5 %collective-permute-start.12 = (f32[16,4,64]{2,0,1:T(8,128)}, f32[16,4,64]{2,0,1:T(8,128)}, u32[]{:S(2)}, u32[]{:S(2)}) collective-permute-start(f32[16,4,64]{2,0,1:T(8,128)} %get-tuple-element.8), channel_id=1, source_target_pairs={{0,1},{1,2},{2,3},{3,4},{4,5},{5,6},{6,7},{7,8},{8,9},{9,10},{10,1... | collective-permute-start | bytes 49160 | tf_op jit(solution)/shard_map/ppermute | solution.py:15
  197.0 21.9 %collective-permute-start.15 = (f32[2,16,64]{2,1,0:T(8,128)}, f32[2,16,64]{2,1,0:T(8,128)}, u32[]{:S(2)}, u32[]{:S(2)}) collective-permute-start(f32[2,16,64]{2,1,0:T(8,128)} %get-tuple-element.20), channel_id=1, source_target_pairs={{0,1},{1,2},{2,3},{3,4},{4,5},{5,6},{6,7},{7,8},{8,9},{9,10},{10,1... | collective-permute-start | bytes 24584 | tf_op jit(solution)/shard_map/ppermute | solution.py:15
  198.9 22.4 %collective-permute-start.18 = (f32[2,16,64]{2,1,0:T(8,128)}, f32[2,16,64]{2,1,0:T(8,128)}, u32[]{:S(2)}, u32[]{:S(2)}) collective-permute-start(f32[2,16,64]{2,1,0:T(8,128)} %get-tuple-element.21), channel_id=1, source_target_pairs={{1,0},{2,1},{3,2},{4,3},{5,4},{6,5},{7,6},{8,7},{9,8},{10,9},{11,1... | collective-permute-start | bytes 24584 | tf_op jit(solution)/shard_map/ppermute | solution.py:15
  206.2 15.1 %copy-start.11 = (f32[16,64,1]{1,0,2:T(8,128)S(1)}, f32[16,64,1]{1,0,2:T(8,128)}, u32[]{:S(2)}) copy-start(f32[16,64,1]{1,0,2:T(8,128)} %copy-done.10) | copy-start | bytes 12292
  206.2 23.5 %copy-start.15 = (s32[1024]{0:T(1024)S(1)}, s32[1024]{0:T(1024)}, u32[]{:S(2)}) copy-start(s32[1024]{0:T(1024)} %copy-done.14) | copy-start | bytes 12292
  218.9 15.2 %collective-permute-start.13 = (f32[16,4,64]{2,0,1:T(8,128)}, f32[16,4,64]{2,0,1:T(8,128)S(1)}, u32[]{:S(2)}, u32[]{:S(2)}) collective-permute-start(f32[16,4,64]{2,0,1:T(8,128)} %get-tuple-element.9), channel_id=1, source_target_pairs={{1,0},{2,1},{3,2},{4,3},{5,4},{6,5},{7,6},{8,7},{9,8},{10,9},{11,1... | collective-permute-start | bytes 49160 | tf_op jit(solution)/shard_map/ppermute | solution.py:15
  222.1 13.4 %collective-permute-start.16 = (f32[3,16,64]{2,1,0:T(8,128)S(1)}, f32[3,16,64]{2,1,0:T(8,128)S(1)}, u32[]{:S(2)}, u32[]{:S(2)}) collective-permute-start(f32[3,16,64]{2,1,0:T(8,128)S(1)} %get-tuple-element.18), channel_id=1, source_target_pairs={{0,1},{1,2},{2,3},{3,4},{4,5},{5,6},{6,7},{7,8},{8,9},{9,10},{10,1... | collective-permute-start | bytes 36872 | tf_op jit(solution)/shard_map/ppermute | solution.py:15
  224.0 11.5 %collective-permute-start.19 = (f32[3,16,64]{2,1,0:T(8,128)S(1)}, f32[3,16,64]{2,1,0:T(8,128)S(1)}, u32[]{:S(2)}, u32[]{:S(2)}) collective-permute-start(f32[3,16,64]{2,1,0:T(8,128)S(1)} %get-tuple-element.19), channel_id=1, source_target_pairs={{1,0},{2,1},{3,2},{4,3},{5,4},{6,5},{7,6},{8,7},{9,8},{10,9},{11,1... | collective-permute-start | bytes 36872 | tf_op jit(solution)/shard_map/ppermute | solution.py:15
  230.3 4.6 %copy-start.13 = (s32[1024]{0:T(1024)S(1)}, s32[1024]{0:T(1024)}, u32[]{:S(2)}) copy-start(s32[1024]{0:T(1024)} %copy-done.12) | copy-start | bytes 12292
  230.3 5.9 %copy-start.6 = (bf16[1,64,192]{1,2,0:T(8,128)(2,1)S(1)}, bf16[1,64,192]{1,2,0:T(8,128)(2,1)}, u32[]{:S(2)}) copy-start(bf16[1,64,192]{1,2,0:T(8,128)(2,1)} %copy-done.5) | copy-start | bytes 73732
  230.3 5.9 %copy-start.19 = (f32[16,64]{1,0:T(8,128)S(1)}, f32[16,64]{1,0:T(8,128)}, u32[]{:S(2)}) copy-start(f32[16,64]{1,0:T(8,128)} %fusion.17) | copy-start | bytes 12292
  230.4 6.1 %copy-start.2 = (bf16[16,64,64]{2,1,0:T(8,128)(2,1)S(1)}, bf16[16,64,64]{2,1,0:T(8,128)(2,1)}, u32[]{:S(2)}) copy-start(bf16[16,64,64]{2,1,0:T(8,128)(2,1)} %param.21) | copy-start | bytes 393220
where the time goes:
time: 254 us; the launch traced here: 253 us
  blocking collectives  123 us (48%)
  starting transfers between devices  56.5 us (22%)
  local copies, waits for them, and re-layouts  51.6 us (20%)
  matrix products  14.8 us (6%)
  other arithmetic  5.39 us (2%)
    all_gather x2, blocking collectives, apply_matrix(): lax.all_gather(block_moment[None], ('gx', 'gy'), axis=0, tiled=True)  70.3 us
    ppermute x20, starting transfers between devices, shifted(): return lax.ppermute(block, axis, route)  56.5 us
    all_gather x2, blocking collectives, apply_matrix(): every_top = lax.all_gather(top_moment[None], 'gx', axis=0, tiled=True)  26.3 us
    psum x2, blocking collectives, apply_matrix(): top_moment = lax.psum(top_term, 'gy')  20.4 us
    gather x2, local copies, waits for them, and re-layouts, shards(): jnp.take(signal, order, axis=1).astype(jnp.bfloat16)  12.4 us
    scatter x1, local copies, waits for them, and re-layouts, shards(): smoothed = empty.at[:, order].set(first.reshape(rhs_count, -1))  11.4 us
    scatter x1, local copies, waits for them, and re-layouts, shards(): twice = empty.at[:, order].set(second.reshape(rhs_count, -1))  11.4 us
    dot_general x2, matrix products, apply_matrix(): jnp.einsum('rlns,lnst->rlt', near_rows, near_tiles, preferred_element_typ...  7.46 us
  transfers between devices with their start and end apart: 20, of which 0 were waited for; matrix products, arithmetic and copies ran while one was open for 13% of the time, Pallas kernels for 0%

commit v1 on v0

--- a/solution.py
+++ b/solution.py
@@ -76,7 +76,16 @@
     top_term = jnp.dot(block_moment, block_transfer[0].astype(jnp.float32), precision=HIGH)
     top_moment = lax.psum(top_term, "gy")
     every_top = lax.all_gather(top_moment[None], "gx", axis=0, tiled=True)
-    every_block = lax.all_gather(block_moment[None], ("gx", "gy"), axis=0, tiled=True)
+    works_start = lambda x_local: jnp.concatenate(
+        jax.lax.all_to_all(
+            jnp.stack([x_local for _ in range(jax.lax.axis_size(("gx", "gy")))], 0),
+            ("gx", "gy"),
+            0,
+            0,
+        ),
+        0,
+    )
+    every_block = works_start(block_moment[None])
     top_field = couple(every_top[top_links[0]], top_coupling[0])
     block_field = couple(every_block[block_links[0]], block_coupling[0]) + spread_down(
         top_field, block_transfer[0]

time: 254 us -> 211 us (0.83)
  blocking collectives: 123 us -> 51.8 us
  starting transfers between devices: 56.5 us -> 73.6 us
  local copies, waits for them, and re-layouts: 51.6 us -> 58.2 us
    all_gather x2 -> x0, blocking collectives: 70.3 us -> none  [apply_matrix(): lax.all_gather(block_moment[None], ('gx', 'gy'), axis=0, tiled=True)]
    all_to_all x0 -> x2, starting transfers between devices: none -> 15 us  [apply_matrix(): jax.lax.all_to_all(jnp.stack([x_local for _ in range(jax.lax.axis_size(('...]
    gather x2, local copies, waits for them, and re-layouts: 12.4 us -> 16.6 us  [shards(): jnp.take(signal, order, axis=1).astype(jnp.bfloat16)]
    unnamed x59 -> x65, local copies, waits for them, and re-layouts: 4.88 us -> 6.56 us
  transfers between devices with their start and end apart: 20 -> 22, of which waited for: 0 -> 0; matrix products, arithmetic and copies ran while one was open for 13% -> 17% of each run, Pallas kernels for 0% -> 0%
where the time goes in v1:
time: 211 us; the launch traced here: 208 us
  starting transfers between devices  73.6 us (35%)
  local copies, waits for them, and re-layouts  58.2 us (28%)
  blocking collectives  51.8 us (25%)
  matrix products  14.8 us (7%)
  other arithmetic  7.83 us (4%)
    ppermute x20, starting transfers between devices, shifted(): return lax.ppermute(block, axis, route)  58.6 us
    all_gather x2, blocking collectives, apply_matrix(): every_top = lax.all_gather(top_moment[None], 'gx', axis=0, tiled=True)  26.3 us
    psum x2, blocking collectives, apply_matrix(): top_moment = lax.psum(top_term, 'gy')  19.5 us
    gather x2, local copies, waits for them, and re-layouts, shards(): jnp.take(signal, order, axis=1).astype(jnp.bfloat16)  16.6 us
    all_to_all x2, starting transfers between devices, apply_matrix(): jax.lax.all_to_all(jnp.stack([x_local for _ in range(jax.lax.axis_size(('...  15 us
    scatter x1, local copies, waits for them, and re-layouts, shards(): smoothed = empty.at[:, order].set(first.reshape(rhs_count, -1))  11.4 us
    scatter x1, local copies, waits for them, and re-layouts, shards(): twice = empty.at[:, order].set(second.reshape(rhs_count, -1))  11.4 us
    dot_general x2, matrix products, apply_matrix(): jnp.einsum('rlns,lnst->rlt', near_rows, near_tiles, preferred_element_typ...  7.43 us
  transfers between devices with their start and end apart: 22, of which 0 were waited for; matrix products, arithmetic and copies ran while one was open for 17% of the time, Pallas kernels for 0%

profile of v1, /device:TPU:4, one launch (start us, length us, event | category | flops | bytes accessed | tf_op | source)
XLA Modules:
  0.0 208.1 jit_solution(11078284941871337612)
XLA Ops:
  0.6 0.8 compare_and_fusion
  1.4 1.3 broadcast_clamp_fusion
  2.8 1.5 copy.38
  4.3 15.0 %gather_fusion = bf16[4096,16]{1,0:T(8,128)(2,1)} fusion(bf16[16,4096]{0,1:T(8,128)(2,1)S(1)} %copy.38, s32[4096]{0:T(1024)S(1)} %get-tuple-element.16), kind=kCustom, calls=%fused_computation | custom fusion | bytes 278528 | tf_op jit(solution)/shard_map/jit(_take)/gather | solution.py:152
  19.3 1.6 copy.39
  21.5 2.8 %collective-permute-start.7 = (f32[1,16,64]{2,1,0:T(8,128)S(1)}, f32[1,16,64]{2,1,0:T(8,128)S(1)}, u32[]{:S(2)}, u32[]{:S(2)}) collective-permute-start(f32[1,16,64]{2,1,0:T(8,128)S(1)} %bitcast.193), channel_id=1, source_target_pairs={{1,0},{2,1},{3,2},{4,3},{5,4},{6,5},{7,6},{8,7},{9,8},{10,9},{11,1... | collective-permute-start | bytes 12296 | tf_op jit(solution)/shard_map/ppermute | solution.py:15
  24.3 1.9 collective-permute-start.4
  26.2 2.6 %collective-permute-start = (bf16[16,2,256]{2,0,1:T(8,128)(2,1)S(1)}, bf16[16,2,256]{2,0,1:T(8,128)(2,1)S(1)}, u32[]{:S(2)}, u32[]{:S(2)}) collective-permute-start(bf16[16,2,256]{2,0,1:T(8,128)(2,1)S(1)} %get-tuple-element.14), channel_id=1, source_target_pairs={{0,1},{1,2},{2,3},{3,4},{4,5},{5,6},{6,7},{7,8},{8,9},{9,10},{10,1... | collective-permute-start | bytes 49160 | tf_op jit(solution)/shard_map/ppermute | solution.py:15
  28.9 3.8 %collective-permute-start.1 = (bf16[16,2,256]{2,0,1:T(8,128)(2,1)S(1)}, bf16[16,2,256]{2,0,1:T(8,128)(2,1)S(1)}, u32[]{:S(2)}, u32[]{:S(2)}) collective-permute-start(bf16[16,2,256]{2,0,1:T(8,128)(2,1)S(1)} %get-tuple-element.15), channel_id=1, source_target_pairs={{1,0},{2,1},{3,2},{4,3},{5,4},{6,5},{7,6},{8,7},{9,8},{10,9},{11,1... | collective-permute-start | bytes 49160 | tf_op jit(solution)/shard_map/ppermute | solution.py:15
  32.7 1.9 collective-permute-start.2
  34.8 3.6 %psum.28 = f32[16,64]{1,0:T(8,128)S(1)} all-reduce(f32[16,64]{1,0:T(8,128)S(1)} %fusion.23), channel_id=1, replica_groups=mesh['gx'=4,'gy'=4,'gz'=2] {'gz'}, use_global_device_ids=true, to_apply=%region_0.1 | all-reduce | flops 1024 | bytes 8192 | tf_op jit(solution)/shard_map/psum | solution.py:69
  38.4 0.8 reshape.287
  39.2 8.2 %all-to-all-start = ((f32[16,1,1024]{2,1,0:T(1,128)}), f32[16,1,1024]{2,1,0:T(1,128)S(1)}, u32[]{:S(2)}, u32[]{:S(2)}) async-start(f32[16,1,1024]{2,1,0:T(1,128)} %reshape.287), calls=%async_computation | async-start | bytes 131072 | tf_op jit(solution)/shard_map/all_to_all | solution.py:80
  48.0 9.1 %psum.29 = f32[1,16,64]{2,1,0:T(8,128)S(1)} all-reduce(f32[1,16,64]{2,1,0:T(8,128)S(1)} %convolution_bitcast_fusion.11), channel_id=1, replica_groups=mesh['gx'=4,'gy'=4,'gz'=2] {'gy'}, use_global_device_ids=true, to_apply=%region_1.2 | all-reduce | flops 1024 | bytes 8192 | tf_op jit(solution)/shard_map/psum | solution.py:77
  57.0 13.1 %all_gather.6 = f32[4,16,64]{2,1,0:T(8,128)S(1)} all-gather(f32[1,16,64]{2,1,0:T(8,128)S(1)} %psum.29), channel_id=1, replica_groups=mesh['gx'=4,'gy'=4,'gz'=2] {'gx'}, dimensions={0}, use_global_device_ids=true | all-gather | bytes 20480 | tf_op jit(solution)/shard_map/all_gather | solution.py:78
  71.1 1.9 collective-permute-start.5
  73.0 4.5 %collective-permute-start.8 = (f32[2,16,64]{2,1,0:T(8,128)S(1)}, f32[2,16,64]{2,1,0:T(8,128)S(1)}, u32[]{:S(2)}, u32[]{:S(2)}) collective-permute-start(f32[2,16,64]{2,1,0:T(8,128)S(1)} %get-tuple-element.25), channel_id=1, source_target_pairs={{1,0},{2,1},{3,2},{4,3},{5,4},{6,5},{7,6},{8,7},{9,8},{10,9},{11,1... | collective-permute-start | bytes 24584 | tf_op jit(solution)/shard_map/ppermute | solution.py:15
  78.3 1.9 collective-permute-start.3
  80.2 2.4 %collective-permute-start.6 = (f32[3,16,64]{2,1,0:T(8,128)S(1)}, f32[3,16,64]{2,1,0:T(8,128)S(1)}, u32[]{:S(2)}, u32[]{:S(2)}) collective-permute-start(f32[3,16,64]{2,1,0:T(8,128)S(1)} %get-tuple-element.22), channel_id=1, source_target_pairs={{0,1},{1,2},{2,3},{3,4},{4,5},{5,6},{6,7},{7,8},{8,9},{9,10},{10,1... | collective-permute-start | bytes 36872 | tf_op jit(solution)/shard_map/ppermute | solution.py:15
  82.7 4.1 %collective-permute-start.9 = (f32[3,16,64]{2,1,0:T(8,128)S(1)}, f32[3,16,64]{2,1,0:T(8,128)S(1)}, u32[]{:S(2)}, u32[]{:S(2)}) collective-permute-start(f32[3,16,64]{2,1,0:T(8,128)S(1)} %get-tuple-element.23), channel_id=1, source_target_pairs={{1,0},{2,1},{3,2},{4,3},{5,4},{6,5},{7,6},{8,7},{9,8},{10,9},{11,1... | collective-permute-start | bytes 36872 | tf_op jit(solution)/shard_map/ppermute | solution.py:15
  86.8 0.6 gather_fusion.1
  87.4 3.7 %convolution_bitcast_fusion.1 = f32[16,16,256]{2,1,0:T(8,128)S(1)} fusion(bf16[16,16,3,256]{3,0,2,1:T(8,128)(2,1)S(1)} %bitcast.178, bf16[16,3,256,256]{3,2,1,0:T(8,128)(2,1)} %param.18), kind=kOutput, calls=%fused_computation.17 | convolution fusion | flops 100663296 | bytes 6946816 | tf_op jit(solution)/shard_map/rlns,lnst->rlt/dot_general | solution.py:110
  91.1 0.6 gather_fusion.2
  91.8 0.6 gather_fusion.3
  92.4 0.6 broadcast.182
  92.9 0.8 reduce
  95.0 0.7 fusion.37
  95.8 0.9 fusion.3
  96.9 0.6 fusion.33
  98.2 1.9 collective-permute-start.17
  100.1 2.4 %collective-permute-start.14 = (f32[1,16,64]{2,1,0:T(8,128)S(1)}, f32[1,16,64]{2,1,0:T(8,128)S(1)}, u32[]{:S(2)}, u32[]{:S(2)}) collective-permute-start(f32[1,16,64]{2,1,0:T(8,128)S(1)} %bitcast.198), channel_id=1, source_target_pairs={{0,1},{1,2},{2,3},{3,4},{4,5},{5,6},{6,7},{7,8},{8,9},{9,10},{10,1... | collective-permute-start | bytes 12296 | tf_op jit(solution)/shard_map/ppermute | solution.py:15
  102.6 0.6 fusion.32
  103.2 2.5 %collective-permute-start.10 = (bf16[16,2,256]{2,0,1:T(8,128)(2,1)}, bf16[16,2,256]{2,0,1:T(8,128)(2,1)}, u32[]{:S(2)}, u32[]{:S(2)}) collective-permute-start(bf16[16,2,256]{2,0,1:T(8,128)(2,1)} %get-tuple-element.10), channel_id=1, source_target_pairs={{0,1},{1,2},{2,3},{3,4},{4,5},{5,6},{6,7},{7,8},{8,9},{9,10},{10,1... | collective-permute-start | bytes 49160 | tf_op jit(solution)/shard_map/ppermute | solution.py:15
  105.7 4.0 %collective-permute-start.11 = (bf16[16,2,256]{2,0,1:T(8,128)(2,1)}, bf16[16,2,256]{2,0,1:T(8,128)(2,1)}, u32[]{:S(2)}, u32[]{:S(2)}) collective-permute-start(bf16[16,2,256]{2,0,1:T(8,128)(2,1)} %get-tuple-element.11), channel_id=1, source_target_pairs={{1,0},{2,1},{3,2},{4,3},{5,4},{6,5},{7,6},{8,7},{9,8},{10,9},{11,1... | collective-permute-start | bytes 49160 | tf_op jit(solution)/shard_map/ppermute | solution.py:15
  109.7 2.5 %psum.30 = f32[16,64]{1,0:T(8,128)S(1)} all-reduce(f32[16,64]{1,0:T(8,128)S(1)} %fusion.19), channel_id=1, replica_groups=mesh['gx'=4,'gy'=4,'gz'=2] {'gz'}, use_global_device_ids=true, to_apply=%region_3.4 | all-reduce | flops 1024 | bytes 8192 | tf_op jit(solution)/shard_map/psum | solution.py:69
  112.3 10.4 %psum.31 = f32[1,16,64]{2,1,0:T(8,128)S(1)} all-reduce(f32[1,16,64]{2,1,0:T(8,128)S(1)} %convolution_bitcast_fusion.7), channel_id=1, replica_groups=mesh['gx'=4,'gy'=4,'gz'=2] {'gy'}, use_global_device_ids=true, to_apply=%region_4.5 | all-reduce | flops 1024 | bytes 8192 | tf_op jit(solution)/shard_map/psum | solution.py:77
  122.7 13.2 %all_gather.7 = f32[4,16,64]{2,1,0:T(8,128)S(1)} all-gather(f32[1,16,64]{2,1,0:T(8,128)S(1)} %psum.31), channel_id=1, replica_groups=mesh['gx'=4,'gy'=4,'gz'=2] {'gx'}, dimensions={0}, use_global_device_ids=true | all-gather | bytes 20480 | tf_op jit(solution)/shard_map/all_gather | solution.py:78
  136.5 0.6 pad_maximum_fusion.13
  137.1 1.9 collective-permute-start.15
  139.0 4.5 %collective-permute-start.18 = (f32[2,16,64]{2,1,0:T(8,128)}, f32[2,16,64]{2,1,0:T(8,128)}, u32[]{:S(2)}, u32[]{:S(2)}) collective-permute-start(f32[2,16,64]{2,1,0:T(8,128)} %get-tuple-element.21), channel_id=1, source_target_pairs={{1,0},{2,1},{3,2},{4,3},{5,4},{6,5},{7,6},{8,7},{9,8},{10,9},{11,1... | collective-permute-start | bytes 24584 | tf_op jit(solution)/shard_map/ppermute | solution.py:15
  143.5 0.8 convolution_bitcast_fusion.6
  144.3 1.9 collective-permute-start.12
  146.2 0.8 reshape.289
  147.0 6.8 %all-to-all-start.1 = ((f32[16,1,1024]{2,1,0:T(1,128)}), f32[16,1,1024]{2,1,0:T(1,128)}, u32[]{:S(2)}, u32[]{:S(2)}) async-start(f32[16,1,1024]{2,1,0:T(1,128)} %reshape.289), calls=%async_computation.1 | async-start | bytes 131072 | tf_op jit(solution)/shard_map/all_to_all | solution.py:80
  153.8 2.0 copy.51
  155.8 11.4 %scatter_custom_fusion = f32[16,4096]{0,1:T(8,128)S(1)} fusion(s32[4096]{0:T(1024)} %get-tuple-element.17, f32[4096,16]{1,0:T(8,128)} %copy.51, f32[]{:T(128)} %constant.15.clone.1), kind=kCustom, calls=%fused_computation.42 | custom fusion | bytes 262656 | tf_op jit(solution)/shard_map/scatter | solution.py:156
  167.2 1.3 copy.58
  168.5 4.9 %collective-permute-start.13 = (f32[16,4,64]{2,0,1:T(8,128)}, f32[16,4,64]{2,0,1:T(8,128)S(1)}, u32[]{:S(2)}, u32[]{:S(2)}) collective-permute-start(f32[16,4,64]{2,0,1:T(8,128)} %get-tuple-element.9), channel_id=1, source_target_pairs={{1,0},{2,1},{3,2},{4,3},{5,4},{6,5},{7,6},{8,7},{9,8},{10,9},{11,1... | collective-permute-start | bytes 49160 | tf_op jit(solution)/shard_map/ppermute | solution.py:15
  173.4 0.8 pad_maximum_fusion.9
  174.1 1.9 collective-permute-start.16
  176.1 4.7 %collective-permute-start.19 = (f32[3,16,64]{2,1,0:T(8,128)S(1)}, f32[3,16,64]{2,1,0:T(8,128)S(1)}, u32[]{:S(2)}, u32[]{:S(2)}) collective-permute-start(f32[3,16,64]{2,1,0:T(8,128)S(1)} %get-tuple-element.19), channel_id=1, source_target_pairs={{1,0},{2,1},{3,2},{4,3},{5,4},{6,5},{7,6},{8,7},{9,8},{10,9},{11,1... | collective-permute-start | bytes 36872 | tf_op jit(solution)/shard_map/ppermute | solution.py:15
  180.8 0.9 pad_maximum_fusion.3
  181.8 0.7 gather_fusion.6
  182.5 3.7 %convolution_bitcast_fusion = f32[16,16,256]{2,1,0:T(8,128)S(1)} fusion(bf16[16,16,3,256]{3,0,2,1:T(8,128)(2,1)S(1)} %bitcast.177, bf16[16,3,256,256]{3,2,1,0:T(8,128)(2,1)} %param.18), kind=kOutput, calls=%fused_computation.15 | convolution fusion | flops 100663296 | bytes 6946816 | tf_op jit(solution)/shard_map/rlns,lnst->rlt/dot_general | solution.py:110
  186.3 0.8 pad_maximum_fusion.1
  187.1 0.6 gather_fusion.7
  187.8 0.7 gather_fusion.8
  188.5 1.6 reduce.1
  190.2 0.7 gather_fusion.9
  191.5 0.7 fusion.39
  192.2 0.9 fusion.4
  193.4 2.0 copy.57
  195.4 11.4 %scatter_custom_fusion.1 = f32[16,4096]{0,1:T(8,128)S(1)} fusion(s32[4096]{0:T(1024)} %get-tuple-element.17, f32[4096,16]{1,0:T(8,128)} %copy.57, f32[]{:T(128)} %constant.15.clone.1), kind=kCustom, calls=%fused_computation.40 | custom fusion | bytes 262656 | tf_op jit(solution)/shard_map/scatter | solution.py:157
  206.8 1.3 copy.59
  (133 shorter events, 6.7 us)
Async XLA Ops:
  0.6 20.3 %copy-start = (bf16[16,64,256]{2,1,0:T(8,128)(2,1)S(1)}, bf16[16,64,256]{2,1,0:T(8,128)(2,1)}, u32[]{:S(2)}) copy-start(bf16[16,64,256]{2,1,0:T(8,128)(2,1)} %param.20) | copy-start | bytes 1572868
  2.8 18.5 %copy-start.1 = (bf16[16,64,64]{2,1,0:T(8,128)(2,1)S(1)}, bf16[16,64,64]{2,1,0:T(8,128)(2,1)}, u32[]{:S(2)}) copy-start(bf16[16,64,64]{2,1,0:T(8,128)(2,1)} %param.21) | copy-start | bytes 393220
  4.2 30.4 %copy-start.10 = (bf16[1,64,64]{2,1,0:T(8,128)(2,1)S(1)}, bf16[1,64,64]{2,1,0:T(8,128)(2,1)}, u32[]{:S(2)}) copy-start(bf16[1,64,64]{2,1,0:T(8,128)(2,1)} %param.24) | copy-start | bytes 24580
  4.3 43.1 %copy-start.24 = (s32[1,3]{1,0:T(1,128)S(1)}, s32[1,3]{1,0:T(1,128)}, u32[]{:S(2)}) copy-start(s32[1,3]{1,0:T(1,128)} %param.26) | copy-start | bytes 40
  4.3 43.1 %copy-start.25 = (s32[1,3]{1,0:T(1,128)S(1)}, s32[1,3]{1,0:T(1,128)}, u32[]{:S(2)}) copy-start(s32[1,3]{1,0:T(1,128)} %param.29) | copy-start | bytes 40
  4.3 43.1 %copy-start.26 = (s32[1,3]{1,0:T(1,128)S(1)}, s32[1,3]{1,0:T(1,128)}, u32[]{:S(2)}) copy-start(s32[1,3]{1,0:T(1,128)} %param.31) | copy-start | bytes 40
  4.3 43.2 %copy-start.22 = (s32[16,3]{0,1:T(4,128)S(1)}, s32[16,3]{0,1:T(4,128)}, u32[]{:S(2)}) copy-start(s32[16,3]{0,1:T(4,128)} %param.23) | copy-start | bytes 580
  4.3 43.2 %copy-start.23 = (s32[16,3]{0,1:T(4,128)S(1)}, s32[16,3]{0,1:T(4,128)}, u32[]{:S(2)}) copy-start(s32[16,3]{0,1:T(4,128)} %param.19) | copy-start | bytes 580
  4.3 43.4 %copy-start.17 = (bf16[1,64,192]{2,1,0:T(8,128)(2,1)S(1)}, bf16[1,64,192]{2,1,0:T(8,128)(2,1)}, u32[]{:S(2)}) copy-start(bf16[1,64,192]{2,1,0:T(8,128)(2,1)} %param.30) | copy-start | bytes 73732
  4.3 43.5 %copy-start.9 = (bf16[1,64,64]{2,1,0:T(8,128)(2,1)S(1)}, bf16[1,64,64]{2,1,0:T(8,128)(2,1)}, u32[]{:S(2)}) copy-start(bf16[1,64,64]{2,1,0:T(8,128)(2,1)} %param.27) | copy-start | bytes 24580
  19.3 58.3 %copy-start.18 = (bf16[1,64,192]{2,1,0:T(8,128)(2,1)S(1)}, bf16[1,64,192]{2,1,0:T(8,128)(2,1)}, u32[]{:S(2)}) copy-start(bf16[1,64,192]{2,1,0:T(8,128)(2,1)} %param.25) | copy-start | bytes 73732
  19.3 58.4 %copy-start.19 = (bf16[1,64,192]{2,1,0:T(8,128)(2,1)S(1)}, bf16[1,64,192]{2,1,0:T(8,128)(2,1)}, u32[]{:S(2)}) copy-start(bf16[1,64,192]{2,1,0:T(8,128)(2,1)} %param.28) | copy-start | bytes 73732
  19.3 58.5 %copy-start.4 = (bf16[16,64,192]{2,1,0:T(8,128)(2,1)S(1)}, bf16[16,64,192]{2,1,0:T(8,128)(2,1)}, u32[]{:S(2)}) copy-start(bf16[16,64,192]{2,1,0:T(8,128)(2,1)} %param.22) | copy-start | bytes 1179652
  21.5 49.6 %collective-permute-start.7 = (f32[1,16,64]{2,1,0:T(8,128)S(1)}, f32[1,16,64]{2,1,0:T(8,128)S(1)}, u32[]{:S(2)}, u32[]{:S(2)}) collective-permute-start(f32[1,16,64]{2,1,0:T(8,128)S(1)} %bitcast.193), channel_id=1, source_target_pairs={{1,0},{2,1},{3,2},{4,3},{5,4},{6,5},{7,6},{8,7},{9,8},{10,9},{11,1... | collective-permute-start | bytes 12296 | tf_op jit(solution)/shard_map/ppermute | solution.py:15
  24.3 46.8 %collective-permute-start.4 = (f32[1,16,64]{2,1,0:T(8,128)S(1)}, f32[1,16,64]{2,1,0:T(8,128)S(1)}, u32[]{:S(2)}, u32[]{:S(2)}) collective-permute-start(f32[1,16,64]{2,1,0:T(8,128)S(1)} %bitcast.194), channel_id=1, source_target_pairs={{0,1},{1,2},{2,3},{3,4},{4,5},{5,6},{6,7},{7,8},{8,9},{9,10},{10,1... | collective-permute-start | bytes 12296 | tf_op jit(solution)/shard_map/ppermute | solution.py:15
  26.2 56.4 %collective-permute-start = (bf16[16,2,256]{2,0,1:T(8,128)(2,1)S(1)}, bf16[16,2,256]{2,0,1:T(8,128)(2,1)S(1)}, u32[]{:S(2)}, u32[]{:S(2)}) collective-permute-start(bf16[16,2,256]{2,0,1:T(8,128)(2,1)S(1)} %get-tuple-element.14), channel_id=1, source_target_pairs={{0,1},{1,2},{2,3},{3,4},{4,5},{5,6},{6,7},{7,8},{8,9},{9,10},{10,1... | collective-permute-start | bytes 49160 | tf_op jit(solution)/shard_map/ppermute | solution.py:15
  28.9 57.8 %collective-permute-start.1 = (bf16[16,2,256]{2,0,1:T(8,128)(2,1)S(1)}, bf16[16,2,256]{2,0,1:T(8,128)(2,1)S(1)}, u32[]{:S(2)}, u32[]{:S(2)}) collective-permute-start(bf16[16,2,256]{2,0,1:T(8,128)(2,1)S(1)} %get-tuple-element.15), channel_id=1, source_target_pairs={{1,0},{2,1},{3,2},{4,3},{5,4},{6,5},{7,6},{8,7},{9,8},{10,9},{11,1... | collective-permute-start | bytes 49160 | tf_op jit(solution)/shard_map/ppermute | solution.py:15
  32.7 58.3 %collective-permute-start.2 = (f32[16,4,64]{2,0,1:T(8,128)S(1)}, f32[16,4,64]{2,0,1:T(8,128)S(1)}, u32[]{:S(2)}, u32[]{:S(2)}) collective-permute-start(f32[16,4,64]{2,0,1:T(8,128)S(1)} %get-tuple-element.12), channel_id=1, source_target_pairs={{0,1},{1,2},{2,3},{3,4},{4,5},{5,6},{6,7},{7,8},{8,9},{9,10},{10,1... | collective-permute-start | bytes 49160 | tf_op jit(solution)/shard_map/ppermute | solution.py:15
  39.2 53.2 %all-to-all-start = ((f32[16,1,1024]{2,1,0:T(1,128)}), f32[16,1,1024]{2,1,0:T(1,128)S(1)}, u32[]{:S(2)}, u32[]{:S(2)}) async-start(f32[16,1,1024]{2,1,0:T(1,128)} %reshape.287), calls=%async_computation | async-start | bytes 131072 | tf_op jit(solution)/shard_map/all_to_all | solution.py:80
  47.5 46.4 %copy-start.20 = (s32[1024]{0:T(1024)}, s32[1024]{0:T(1024)S(1)}, u32[]{:S(2)}) copy-start(s32[1024]{0:T(1024)S(1)} %pad_clamp_fusion.1) | copy-start | bytes 12292
  47.5 44.3 %copy-start.21 = (s32[1024]{0:T(1024)}, s32[1024]{0:T(1024)S(1)}, u32[]{:S(2)}) copy-start(s32[1024]{0:T(1024)S(1)} %pad_clamp_fusion.2) | copy-start | bytes 12292
  70.9 20.2 %copy-start.13 = (s32[1024]{0:T(1024)}, s32[1024]{0:T(1024)S(1)}, u32[]{:S(2)}) copy-start(s32[1024]{0:T(1024)S(1)} %pad_clamp_fusion.3) | copy-start | bytes 12292
  71.1 7.2 %collective-permute-start.5 = (f32[2,16,64]{2,1,0:T(8,128)S(1)}, f32[2,16,64]{2,1,0:T(8,128)S(1)}, u32[]{:S(2)}, u32[]{:S(2)}) collective-permute-start(f32[2,16,64]{2,1,0:T(8,128)S(1)} %get-tuple-element.24), channel_id=1, source_target_pairs={{0,1},{1,2},{2,3},{3,4},{4,5},{5,6},{6,7},{7,8},{8,9},{9,10},{10,1... | collective-permute-start | bytes 24584 | tf_op jit(solution)/shard_map/ppermute | solution.py:15
  73.0 7.2 %collective-permute-start.8 = (f32[2,16,64]{2,1,0:T(8,128)S(1)}, f32[2,16,64]{2,1,0:T(8,128)S(1)}, u32[]{:S(2)}, u32[]{:S(2)}) collective-permute-start(f32[2,16,64]{2,1,0:T(8,128)S(1)} %get-tuple-element.25), channel_id=1, source_target_pairs={{1,0},{2,1},{3,2},{4,3},{5,4},{6,5},{7,6},{8,7},{9,8},{10,9},{11,1... | collective-permute-start | bytes 24584 | tf_op jit(solution)/shard_map/ppermute | solution.py:15
  77.6 13.5 %copy-start.15 = (s32[1024]{0:T(1024)}, s32[1024]{0:T(1024)S(1)}, u32[]{:S(2)}) copy-start(s32[1024]{0:T(1024)S(1)} %pad_clamp_fusion.4) | copy-start | bytes 12292
  77.7 17.1 %copy-start.7 = (bf16[1,64,192]{1,2,0:T(8,128)(2,1)}, bf16[1,64,192]{1,2,0:T(8,128)(2,1)S(1)}, u32[]{:S(2)}) copy-start(bf16[1,64,192]{1,2,0:T(8,128)(2,1)S(1)} %copy.44) | copy-start | bytes 73732
  77.9 16.5 %copy-start.5 = (bf16[1,64,192]{1,2,0:T(8,128)(2,1)}, bf16[1,64,192]{1,2,0:T(8,128)(2,1)S(1)}, u32[]{:S(2)}) copy-start(bf16[1,64,192]{1,2,0:T(8,128)(2,1)S(1)} %copy.46) | copy-start | bytes 73732
  78.3 12.8 %collective-permute-start.3 = (f32[16,4,64]{2,0,1:T(8,128)S(1)}, f32[16,4,64]{2,0,1:T(8,128)S(1)}, u32[]{:S(2)}, u32[]{:S(2)}) collective-permute-start(f32[16,4,64]{2,0,1:T(8,128)S(1)} %get-tuple-element.13), channel_id=1, source_target_pairs={{1,0},{2,1},{3,2},{4,3},{5,4},{6,5},{7,6},{8,7},{9,8},{10,9},{11,1... | collective-permute-start | bytes 49160 | tf_op jit(solution)/shard_map/ppermute | solution.py:15
  80.2 11.5 %collective-permute-start.6 = (f32[3,16,64]{2,1,0:T(8,128)S(1)}, f32[3,16,64]{2,1,0:T(8,128)S(1)}, u32[]{:S(2)}, u32[]{:S(2)}) collective-permute-start(f32[3,16,64]{2,1,0:T(8,128)S(1)} %get-tuple-element.22), channel_id=1, source_target_pairs={{0,1},{1,2},{2,3},{3,4},{4,5},{5,6},{6,7},{7,8},{8,9},{9,10},{10,1... | collective-permute-start | bytes 36872 | tf_op jit(solution)/shard_map/ppermute | solution.py:15
  82.7 9.1 %collective-permute-start.9 = (f32[3,16,64]{2,1,0:T(8,128)S(1)}, f32[3,16,64]{2,1,0:T(8,128)S(1)}, u32[]{:S(2)}, u32[]{:S(2)}) collective-permute-start(f32[3,16,64]{2,1,0:T(8,128)S(1)} %get-tuple-element.23), channel_id=1, source_target_pairs={{1,0},{2,1},{3,2},{4,3},{5,4},{6,5},{7,6},{8,7},{9,8},{10,9},{11,1... | collective-permute-start | bytes 36872 | tf_op jit(solution)/shard_map/ppermute | solution.py:15
  96.9 58.9 %copy-start.3 = (bf16[16,16,256]{2,0,1:T(8,128)(2,1)}, bf16[16,16,256]{2,0,1:T(8,128)(2,1)S(1)}, u32[]{:S(2)}) copy-start(bf16[16,16,256]{2,0,1:T(8,128)(2,1)S(1)} %get-tuple-element.26) | copy-start | bytes 393220
  98.1 57.7 %copy-start.12 = (f32[16,64,1]{1,0,2:T(8,128)}, f32[16,64,1]{1,0,2:T(8,128)S(1)}, u32[]{:S(2)}) copy-start(f32[16,64,1]{1,0,2:T(8,128)S(1)} %fusion.38) | copy-start | bytes 12292
  98.2 38.2 %collective-permute-start.17 = (f32[1,16,64]{2,1,0:T(8,128)S(1)}, f32[1,16,64]{2,1,0:T(8,128)S(1)}, u32[]{:S(2)}, u32[]{:S(2)}) collective-permute-start(f32[1,16,64]{2,1,0:T(8,128)S(1)} %bitcast.197), channel_id=1, source_target_pairs={{1,0},{2,1},{3,2},{4,3},{5,4},{6,5},{7,6},{8,7},{9,8},{10,9},{11,1... | collective-permute-start | bytes 12296 | tf_op jit(solution)/shard_map/ppermute | solution.py:15
  100.1 36.3 %collective-permute-start.14 = (f32[1,16,64]{2,1,0:T(8,128)S(1)}, f32[1,16,64]{2,1,0:T(8,128)S(1)}, u32[]{:S(2)}, u32[]{:S(2)}) collective-permute-start(f32[1,16,64]{2,1,0:T(8,128)S(1)} %bitcast.198), channel_id=1, source_target_pairs={{0,1},{1,2},{2,3},{3,4},{4,5},{5,6},{6,7},{7,8},{8,9},{9,10},{10,1... | collective-permute-start | bytes 12296 | tf_op jit(solution)/shard_map/ppermute | solution.py:15
  103.2 72.8 %collective-permute-start.10 = (bf16[16,2,256]{2,0,1:T(8,128)(2,1)}, bf16[16,2,256]{2,0,1:T(8,128)(2,1)}, u32[]{:S(2)}, u32[]{:S(2)}) collective-permute-start(bf16[16,2,256]{2,0,1:T(8,128)(2,1)} %get-tuple-element.10), channel_id=1, source_target_pairs={{0,1},{1,2},{2,3},{3,4},{4,5},{5,6},{6,7},{7,8},{8,9},{9,10},{10,1... | collective-permute-start | bytes 49160 | tf_op jit(solution)/shard_map/ppermute | solution.py:15
  105.7 75.1 %collective-permute-start.11 = (bf16[16,2,256]{2,0,1:T(8,128)(2,1)}, bf16[16,2,256]{2,0,1:T(8,128)(2,1)}, u32[]{:S(2)}, u32[]{:S(2)}) collective-permute-start(bf16[16,2,256]{2,0,1:T(8,128)(2,1)} %get-tuple-element.11), channel_id=1, source_target_pairs={{1,0},{2,1},{3,2},{4,3},{5,4},{6,5},{7,6},{8,7},{9,8},{10,9},{11,1... | collective-permute-start | bytes 49160 | tf_op jit(solution)/shard_map/ppermute | solution.py:15
  137.1 31.4 %collective-permute-start.15 = (f32[2,16,64]{2,1,0:T(8,128)}, f32[2,16,64]{2,1,0:T(8,128)}, u32[]{:S(2)}, u32[]{:S(2)}) collective-permute-start(f32[2,16,64]{2,1,0:T(8,128)} %get-tuple-element.20), channel_id=1, source_target_pairs={{0,1},{1,2},{2,3},{3,4},{4,5},{5,6},{6,7},{7,8},{8,9},{9,10},{10,1... | collective-permute-start | bytes 24584 | tf_op jit(solution)/shard_map/ppermute | solution.py:15
  139.0 34.4 %collective-permute-start.18 = (f32[2,16,64]{2,1,0:T(8,128)}, f32[2,16,64]{2,1,0:T(8,128)}, u32[]{:S(2)}, u32[]{:S(2)}) collective-permute-start(f32[2,16,64]{2,1,0:T(8,128)} %get-tuple-element.21), channel_id=1, source_target_pairs={{1,0},{2,1},{3,2},{4,3},{5,4},{6,5},{7,6},{8,7},{9,8},{10,9},{11,1... | collective-permute-start | bytes 24584 | tf_op jit(solution)/shard_map/ppermute | solution.py:15
  144.3 41.9 %collective-permute-start.12 = (f32[16,4,64]{2,0,1:T(8,128)}, f32[16,4,64]{2,0,1:T(8,128)}, u32[]{:S(2)}, u32[]{:S(2)}) collective-permute-start(f32[16,4,64]{2,0,1:T(8,128)} %get-tuple-element.8), channel_id=1, source_target_pairs={{0,1},{1,2},{2,3},{3,4},{4,5},{5,6},{6,7},{7,8},{8,9},{9,10},{10,1... | collective-permute-start | bytes 49160 | tf_op jit(solution)/shard_map/ppermute | solution.py:15
  147.0 41.5 %all-to-all-start.1 = ((f32[16,1,1024]{2,1,0:T(1,128)}), f32[16,1,1024]{2,1,0:T(1,128)}, u32[]{:S(2)}, u32[]{:S(2)}) async-start(f32[16,1,1024]{2,1,0:T(1,128)} %reshape.289), calls=%async_computation.1 | async-start | bytes 131072 | tf_op jit(solution)/shard_map/all_to_all | solution.py:80
  168.5 17.8 %collective-permute-start.13 = (f32[16,4,64]{2,0,1:T(8,128)}, f32[16,4,64]{2,0,1:T(8,128)S(1)}, u32[]{:S(2)}, u32[]{:S(2)}) collective-permute-start(f32[16,4,64]{2,0,1:T(8,128)} %get-tuple-element.9), channel_id=1, source_target_pairs={{1,0},{2,1},{3,2},{4,3},{5,4},{6,5},{7,6},{8,7},{9,8},{10,9},{11,1... | collective-permute-start | bytes 49160 | tf_op jit(solution)/shard_map/ppermute | solution.py:15
  174.1 13.6 %collective-permute-start.16 = (f32[3,16,64]{2,1,0:T(8,128)S(1)}, f32[3,16,64]{2,1,0:T(8,128)S(1)}, u32[]{:S(2)}, u32[]{:S(2)}) collective-permute-start(f32[3,16,64]{2,1,0:T(8,128)S(1)} %get-tuple-element.18), channel_id=1, source_target_pairs={{0,1},{1,2},{2,3},{3,4},{4,5},{5,6},{6,7},{7,8},{8,9},{9,10},{10,1... | collective-permute-start | bytes 36872 | tf_op jit(solution)/shard_map/ppermute | solution.py:15
  176.1 11.7 %collective-permute-start.19 = (f32[3,16,64]{2,1,0:T(8,128)S(1)}, f32[3,16,64]{2,1,0:T(8,128)S(1)}, u32[]{:S(2)}, u32[]{:S(2)}) collective-permute-start(f32[3,16,64]{2,1,0:T(8,128)S(1)} %get-tuple-element.19), channel_id=1, source_target_pairs={{1,0},{2,1},{3,2},{4,3},{5,4},{6,5},{7,6},{8,7},{9,8},{10,9},{11,1... | collective-permute-start | bytes 36872 | tf_op jit(solution)/shard_map/ppermute | solution.py:15
  182.5 4.6 %copy-start.14 = (s32[1024]{0:T(1024)S(1)}, s32[1024]{0:T(1024)}, u32[]{:S(2)}) copy-start(s32[1024]{0:T(1024)} %copy-done.13) | copy-start | bytes 12292
  182.5 8.4 %copy-start.6 = (bf16[1,64,192]{1,2,0:T(8,128)(2,1)S(1)}, bf16[1,64,192]{1,2,0:T(8,128)(2,1)}, u32[]{:S(2)}) copy-start(bf16[1,64,192]{1,2,0:T(8,128)(2,1)} %copy-done.5) | copy-start | bytes 73732
  186.2 4.8 %copy-start.16 = (f32[16,64]{1,0:T(8,128)S(1)}, f32[16,64]{1,0:T(8,128)}, u32[]{:S(2)}) copy-start(f32[16,64]{1,0:T(8,128)} %convolution_bitcast_fusion.6) | copy-start | bytes 12292
  186.2 4.9 %copy-start.11 = (bf16[1,64,64]{2,1,0:T(8,128)(2,1)S(1)}, bf16[1,64,64]{2,1,0:T(8,128)(2,1)}, u32[]{:S(2)}) copy-start(bf16[1,64,64]{2,1,0:T(8,128)(2,1)} %param.24) | copy-start | bytes 24580
  186.2 5.1 %copy-start.8 = (bf16[1,64,192]{1,2,0:T(8,128)(2,1)S(1)}, bf16[1,64,192]{1,2,0:T(8,128)(2,1)}, u32[]{:S(2)}) copy-start(bf16[1,64,192]{1,2,0:T(8,128)(2,1)} %copy-done.7) | copy-start | bytes 73732
  186.2 5.3 %copy-start.2 = (bf16[16,64,64]{2,1,0:T(8,128)(2,1)S(1)}, bf16[16,64,64]{2,1,0:T(8,128)(2,1)}, u32[]{:S(2)}) copy-start(bf16[16,64,64]{2,1,0:T(8,128)(2,1)} %param.21) | copy-start | bytes 393220
